TPU v7x, 32 devices: a whole 2x2x4 slice. The times are simulated.
32 devices in a mesh: seq: 32 (over z, y, x, core).
Axes of the slice: x: 2, y: 2, z: 4, core: 2. Of those that a mesh axis runs over, the one named last changes fastest.
Arguments:
- right_side: bfloat16 [16384, 384], P('seq'), may hold values from -6 to 6
- leaf_inverse: bfloat16 [32, 512, 512], P('seq'), may hold values from -1 to 2
- project_rows: bfloat16 [5, 16384, 128], P(None, 'seq'), may hold values from -3 to 3, as said below
- spread_rows: bfloat16 [5, 16384, 128], P(None, 'seq'), may hold values from -0.119628906 to 0.119628906
- capacity: bfloat16 [5, 4096, 256], P(None, 'seq'), may hold values from -1 to 2, as said below
Outputs:
- solution: float32 [16384, 384], P('seq')
Inputs may be any that keep to these rules, and one draw needn't show every extreme that they name: Rows of project_rows of level l have a scale falling as (2 ** l * 512) ** -0.5. `capacity`: at level l the 128 x 2 * 128 blocks of all devices in one half of a node of 2 ** (l + 1) devices are equal.
All inputs are finite; a program needn't handle non-finite values.
Results may differ from a plain program's by a relative error of at most 0.0095.
Values may be sent and summed in bfloat16 or wider, within the bound.
A program may use at most 64 MiB of HBM per device.

v0:
```python
import jax
import jax.numpy as jnp
from jax import lax
from jax.sharding import PartitionSpec as P


def partner(value, axis, bit):
    mask = 2**bit
    pairs = [(source, source ^ mask) for source in range(lax.axis_size(axis))]
    return lax.ppermute(value, axis, pairs)


def pair_sums(partial_sum, tree_level, half_side):
    for bit_index in range(tree_level):
        partial_sum = partial_sum + partner(partial_sum, "seq", bit_index)
    own_sums = partial_sum.astype(jnp.bfloat16)
    partner_sums = partner(own_sums, "seq", tree_level)
    return jnp.where(
        half_side == 0,
        jnp.concatenate([own_sums, partner_sums], 0),
        jnp.concatenate([partner_sums, own_sums], 0),
    )


def on_device(right_side, leaf_inverse, project_rows, spread_rows, capacity):
    solution = jnp.dot(leaf_inverse[0], right_side, preferred_element_type=jnp.float32)
    device_index = lax.axis_index("seq")
    level_count = project_rows.shape[0]
    for tree_level in range(level_count):
        rounded = solution.astype(jnp.bfloat16)
        partial_sum = jnp.einsum(
            "sr,sk->rk", project_rows[tree_level], rounded, preferred_element_type=jnp.float32
        )
        half_side = device_index >> tree_level & 1
        stacked = pair_sums(partial_sum, tree_level, half_side)
        coefficients = jnp.dot(
            capacity[tree_level], stacked, preferred_element_type=jnp.float32
        ).astype(jnp.bfloat16)
        solution = solution - jnp.dot(
            spread_rows[tree_level], coefficients, preferred_element_type=jnp.float32
        )
    return solution


def solution(mesh):
    return jax.shard_map(
        on_device,
        mesh=mesh,
        in_specs=(
            P("seq", None),
            P("seq", None, None),
            P(None, "seq", None),
            P(None, "seq", None),
            P(None, "seq", None),
        ),
        out_specs=P("seq", None),
        check_vma=False,
    )
```

profile of v0, /device:TPU:0, one launch (start us, length us, event | category | flops | bytes accessed | tf_op | source)
XLA Modules:
  0.0 80.4 jit_solution(12814419477773191705)
XLA Ops:
  0.0 1.0 %copy-done = bf16[1,512,512]{2,1,0:T(8,128)(2,1)S(1)} copy-done((bf16[1,512,512]{2,1,0:T(8,128)(2,1)S(1)}, bf16[1,512,512]{2,1,0:T(8,128)(2,1)}, u32[]{:S(2)}) %copy-start) | copy-done | bytes 524312
  1.0 1.4 %fusion.6 = f32[512,384]{1,0:T(8,128)S(1)} fusion(bf16[512,384]{1,0:T(8,128)(2,1)} %param.5, bf16[1,512,512]{2,1,0:T(8,128)(2,1)S(1)} %copy-done), kind=kOutput, calls=%fused_computation.21 | convolution fusion | flops 201326592 | bytes 1703936 | tf_op jit(solution)/shard_map/dot_general | solution.py:26
  3.3 1.1 %collective-permute-done = bf16[128,384]{1,0:T(8,128)(2,1)} collective-permute-done((bf16[128,384]{1,0:T(8,128)(2,1)S(1)}, bf16[128,384]{1,0:T(8,128)(2,1)}, u32[]{:S(2)}, u32[]{:S(2)}) %collective-permute-start) | collective-permute-done | bytes 98336 | tf_op jit(solution)/shard_map/ppermute | solution.py:10
  4.4 1.5 %fusion.4 = f32[512,384]{1,0:T(8,128)S(1)} fusion(f32[512,384]{1,0:T(8,128)S(1)} %fusion.6, bf16[128,384]{1,0:T(8,128)(2,1)} %collective-permute-done, bf16[128,384]{1,0:T(8,128)(2,1)S(1)} %fusion.5, pred[]{:T(512)S(6)} %eq.15, bf16[5,512,128]{2,1,0:T(8,128)(2,1)S(1)} %copy-done.1, bf16[5,128,256]{2,1,0:T(8,128)(2,1)} %param.9), kind=kOutput, calls=%fused_computation.9 | convolution fusion | flops 76627968 | bytes 1966081 | tf_op jit(solution)/shard_map/dot_general | solution.py:39
  6.6 1.1 %collective-permute-done.1 = f32[128,384]{1,0:T(8,128)S(1)} collective-permute-done((f32[128,384]{1,0:T(8,128)S(1)}, f32[128,384]{1,0:T(8,128)S(1)}, u32[]{:S(2)}, u32[]{:S(2)}) %collective-permute-start.1) | collective-permute-done | bytes 196640 | tf_op jit(solution)/shard_map/ppermute | solution.py:10
  7.7 2.9 %collective-permute-start.2 = (bf16[128,384]{1,0:T(8,128)(2,1)S(1)}, bf16[128,384]{1,0:T(8,128)(2,1)}, u32[]{:S(2)}, u32[]{:S(2)}) collective-permute-start(bf16[128,384]{1,0:T(8,128)(2,1)S(1)} %add_convert_fusion.3), channel_id=1, source_target_pairs={{0,2},{1,3},{2,0},{3,1},{4,6},{5,7},{6,4},{7,5},{8,10},{9,11},{10,... | collective-permute-start | bytes 294920 | tf_op jit(solution)/shard_map/ppermute | solution.py:10
  10.6 3.2 %collective-permute-done.2 = bf16[128,384]{1,0:T(8,128)(2,1)} collective-permute-done((bf16[128,384]{1,0:T(8,128)(2,1)S(1)}, bf16[128,384]{1,0:T(8,128)(2,1)}, u32[]{:S(2)}, u32[]{:S(2)}) %collective-permute-start.2) | collective-permute-done | bytes 98336 | tf_op jit(solution)/shard_map/ppermute | solution.py:10
  13.8 1.5 %fusion.3 = f32[512,384]{1,0:T(8,128)S(1)} fusion(f32[512,384]{1,0:T(8,128)S(1)} %fusion.4, bf16[128,384]{1,0:T(8,128)(2,1)} %collective-permute-done.2, bf16[128,384]{1,0:T(8,128)(2,1)S(1)} %add_convert_fusion.3, pred[]{:T(512)S(6)} %eq.16, bf16[5,512,128]{2,1,0:T(8,128)(2,1)S(1)} %copy-done.1, bf16[5,128,256]{2,1,0:T(8,128)(2,1)} %param.9), kind=kOutput, calls=%fused_computation.7 | convolution fusion | flops 76627968 | bytes 1966081 | tf_op jit(solution)/shard_map/dot_general | solution.py:39
  15.7 1.4 %collective-permute-done.3 = f32[128,384]{1,0:T(8,128)S(1)} collective-permute-done((f32[128,384]{1,0:T(8,128)S(1)}, f32[128,384]{1,0:T(8,128)S(1)}, u32[]{:S(2)}, u32[]{:S(2)}) %collective-permute-start.3) | collective-permute-done | bytes 196640 | tf_op jit(solution)/shard_map/ppermute | solution.py:10
  17.1 1.8 %collective-permute-start.4 = (f32[128,384]{1,0:T(8,128)S(1)}, f32[128,384]{1,0:T(8,128)S(1)}, u32[]{:S(2)}, u32[]{:S(2)}) collective-permute-start(f32[128,384]{1,0:T(8,128)S(1)} %add.31), channel_id=1, source_target_pairs={{0,2},{1,3},{2,0},{3,1},{4,6},{5,7},{6,4},{7,5},{8,10},{9,11},{10,... | collective-permute-start | bytes 589832 | tf_op jit(solution)/shard_map/ppermute | solution.py:10
  18.9 5.2 %collective-permute-done.4 = f32[128,384]{1,0:T(8,128)S(1)} collective-permute-done((f32[128,384]{1,0:T(8,128)S(1)}, f32[128,384]{1,0:T(8,128)S(1)}, u32[]{:S(2)}, u32[]{:S(2)}) %collective-permute-start.4) | collective-permute-done | bytes 196640 | tf_op jit(solution)/shard_map/ppermute | solution.py:10
  24.2 1.8 %collective-permute-start.5 = (bf16[128,384]{1,0:T(8,128)(2,1)S(1)}, bf16[128,384]{1,0:T(8,128)(2,1)}, u32[]{:S(2)}, u32[]{:S(2)}) collective-permute-start(bf16[128,384]{1,0:T(8,128)(2,1)S(1)} %add_convert_fusion.2), channel_id=1, source_target_pairs={{0,4},{1,5},{2,6},{3,7},{4,0},{5,1},{6,2},{7,3},{8,12},{9,13},{10,... | collective-permute-start | bytes 294920 | tf_op jit(solution)/shard_map/ppermute | solution.py:10
  26.0 3.0 %collective-permute-done.5 = bf16[128,384]{1,0:T(8,128)(2,1)} collective-permute-done((bf16[128,384]{1,0:T(8,128)(2,1)S(1)}, bf16[128,384]{1,0:T(8,128)(2,1)}, u32[]{:S(2)}, u32[]{:S(2)}) %collective-permute-start.5) | collective-permute-done | bytes 98336 | tf_op jit(solution)/shard_map/ppermute | solution.py:10
  28.9 1.5 %fusion.2 = f32[512,384]{1,0:T(8,128)S(1)} fusion(f32[512,384]{1,0:T(8,128)S(1)} %fusion.3, bf16[128,384]{1,0:T(8,128)(2,1)} %collective-permute-done.5, bf16[128,384]{1,0:T(8,128)(2,1)S(1)} %add_convert_fusion.2, pred[]{:T(512)S(6)} %eq.17, bf16[5,512,128]{2,1,0:T(8,128)(2,1)S(1)} %copy-done.1, bf16[5,128,256]{2,1,0:T(8,128)(2,1)} %param.9), kind=kOutput, calls=%fused_computation.5 | convolution fusion | flops 76627968 | bytes 1966081 | tf_op jit(solution)/shard_map/dot_general | solution.py:39
  30.8 1.4 %collective-permute-done.6 = f32[128,384]{1,0:T(8,128)S(1)} collective-permute-done((f32[128,384]{1,0:T(8,128)S(1)}, f32[128,384]{1,0:T(8,128)S(1)}, u32[]{:S(2)}, u32[]{:S(2)}) %collective-permute-start.6) | collective-permute-done | bytes 196640 | tf_op jit(solution)/shard_map/ppermute | solution.py:10
  32.2 1.8 %collective-permute-start.7 = (f32[128,384]{1,0:T(8,128)S(1)}, f32[128,384]{1,0:T(8,128)S(1)}, u32[]{:S(2)}, u32[]{:S(2)}) collective-permute-start(f32[128,384]{1,0:T(8,128)S(1)} %add.33), channel_id=1, source_target_pairs={{0,2},{1,3},{2,0},{3,1},{4,6},{5,7},{6,4},{7,5},{8,10},{9,11},{10,... | collective-permute-start | bytes 589832 | tf_op jit(solution)/shard_map/ppermute | solution.py:10
  34.0 5.2 %collective-permute-done.7 = f32[128,384]{1,0:T(8,128)S(1)} collective-permute-done((f32[128,384]{1,0:T(8,128)S(1)}, f32[128,384]{1,0:T(8,128)S(1)}, u32[]{:S(2)}, u32[]{:S(2)}) %collective-permute-start.7) | collective-permute-done | bytes 196640 | tf_op jit(solution)/shard_map/ppermute | solution.py:10
  39.3 1.8 %collective-permute-start.8 = (f32[128,384]{1,0:T(8,128)S(1)}, f32[128,384]{1,0:T(8,128)S(1)}, u32[]{:S(2)}, u32[]{:S(2)}) collective-permute-start(f32[128,384]{1,0:T(8,128)S(1)} %add.34), channel_id=1, source_target_pairs={{0,4},{1,5},{2,6},{3,7},{4,0},{5,1},{6,2},{7,3},{8,12},{9,13},{10,... | collective-permute-start | bytes 589832 | tf_op jit(solution)/shard_map/ppermute | solution.py:10
  41.1 4.3 %collective-permute-done.8 = f32[128,384]{1,0:T(8,128)S(1)} collective-permute-done((f32[128,384]{1,0:T(8,128)S(1)}, f32[128,384]{1,0:T(8,128)S(1)}, u32[]{:S(2)}, u32[]{:S(2)}) %collective-permute-start.8) | collective-permute-done | bytes 196640 | tf_op jit(solution)/shard_map/ppermute | solution.py:10
  45.5 1.9 %collective-permute-start.9 = (bf16[128,384]{1,0:T(8,128)(2,1)S(1)}, bf16[128,384]{1,0:T(8,128)(2,1)}, u32[]{:S(2)}, u32[]{:S(2)}) collective-permute-start(bf16[128,384]{1,0:T(8,128)(2,1)S(1)} %add_convert_fusion.1), channel_id=1, source_target_pairs={{0,8},{1,9},{2,10},{3,11},{4,12},{5,13},{6,14},{7,15},{8,0},{9,1},... | collective-permute-start | bytes 294920 | tf_op jit(solution)/shard_map/ppermute | solution.py:10
  47.3 2.9 %collective-permute-done.9 = bf16[128,384]{1,0:T(8,128)(2,1)} collective-permute-done((bf16[128,384]{1,0:T(8,128)(2,1)S(1)}, bf16[128,384]{1,0:T(8,128)(2,1)}, u32[]{:S(2)}, u32[]{:S(2)}) %collective-permute-start.9) | collective-permute-done | bytes 98336 | tf_op jit(solution)/shard_map/ppermute | solution.py:10
  50.3 1.5 %fusion.1 = f32[512,384]{1,0:T(8,128)S(1)} fusion(f32[512,384]{1,0:T(8,128)S(1)} %fusion.2, bf16[128,384]{1,0:T(8,128)(2,1)} %collective-permute-done.9, bf16[128,384]{1,0:T(8,128)(2,1)S(1)} %add_convert_fusion.1, pred[]{:T(512)S(6)} %eq.18, bf16[5,512,128]{2,1,0:T(8,128)(2,1)S(1)} %copy-done.1, bf16[5,128,256]{2,1,0:T(8,128)(2,1)} %param.9), kind=kOutput, calls=%fused_computation.3 | convolution fusion | flops 76627968 | bytes 1966081 | tf_op jit(solution)/shard_map/dot_general | solution.py:39
  52.1 1.4 %collective-permute-done.10 = f32[128,384]{1,0:T(8,128)S(1)} collective-permute-done((f32[128,384]{1,0:T(8,128)S(1)}, f32[128,384]{1,0:T(8,128)S(1)}, u32[]{:S(2)}, u32[]{:S(2)}) %collective-permute-start.10) | collective-permute-done | bytes 196640 | tf_op jit(solution)/shard_map/ppermute | solution.py:10
  53.6 1.8 %collective-permute-start.11 = (f32[128,384]{1,0:T(8,128)S(1)}, f32[128,384]{1,0:T(8,128)S(1)}, u32[]{:S(2)}, u32[]{:S(2)}) collective-permute-start(f32[128,384]{1,0:T(8,128)S(1)} %add.36), channel_id=1, source_target_pairs={{0,2},{1,3},{2,0},{3,1},{4,6},{5,7},{6,4},{7,5},{8,10},{9,11},{10,... | collective-permute-start | bytes 589832 | tf_op jit(solution)/shard_map/ppermute | solution.py:10
  55.3 5.2 %collective-permute-done.11 = f32[128,384]{1,0:T(8,128)S(1)} collective-permute-done((f32[128,384]{1,0:T(8,128)S(1)}, f32[128,384]{1,0:T(8,128)S(1)}, u32[]{:S(2)}, u32[]{:S(2)}) %collective-permute-start.11) | collective-permute-done | bytes 196640 | tf_op jit(solution)/shard_map/ppermute | solution.py:10
  60.6 1.8 %collective-permute-start.12 = (f32[128,384]{1,0:T(8,128)S(1)}, f32[128,384]{1,0:T(8,128)S(1)}, u32[]{:S(2)}, u32[]{:S(2)}) collective-permute-start(f32[128,384]{1,0:T(8,128)S(1)} %add.37), channel_id=1, source_target_pairs={{0,4},{1,5},{2,6},{3,7},{4,0},{5,1},{6,2},{7,3},{8,12},{9,13},{10,... | collective-permute-start | bytes 589832 | tf_op jit(solution)/shard_map/ppermute | solution.py:10
  62.4 4.3 %collective-permute-done.12 = f32[128,384]{1,0:T(8,128)S(1)} collective-permute-done((f32[128,384]{1,0:T(8,128)S(1)}, f32[128,384]{1,0:T(8,128)S(1)}, u32[]{:S(2)}, u32[]{:S(2)}) %collective-permute-start.12) | collective-permute-done | bytes 196640 | tf_op jit(solution)/shard_map/ppermute | solution.py:10
  66.8 1.9 %collective-permute-start.13 = (f32[128,384]{1,0:T(8,128)S(1)}, f32[128,384]{1,0:T(8,128)S(1)}, u32[]{:S(2)}, u32[]{:S(2)}) collective-permute-start(f32[128,384]{1,0:T(8,128)S(1)} %add.38), channel_id=1, source_target_pairs={{0,8},{1,9},{2,10},{3,11},{4,12},{5,13},{6,14},{7,15},{8,0},{9,1},... | collective-permute-start | bytes 589832 | tf_op jit(solution)/shard_map/ppermute | solution.py:10
  68.6 3.9 %collective-permute-done.13 = f32[128,384]{1,0:T(8,128)S(1)} collective-permute-done((f32[128,384]{1,0:T(8,128)S(1)}, f32[128,384]{1,0:T(8,128)S(1)}, u32[]{:S(2)}, u32[]{:S(2)}) %collective-permute-start.13) | collective-permute-done | bytes 196640 | tf_op jit(solution)/shard_map/ppermute | solution.py:10
  72.5 3.0 %collective-permute-start.14 = (bf16[128,384]{1,0:T(8,128)(2,1)S(1)}, bf16[128,384]{1,0:T(8,128)(2,1)S(1)}, u32[]{:S(2)}, u32[]{:S(2)}) collective-permute-start(bf16[128,384]{1,0:T(8,128)(2,1)S(1)} %add_convert_fusion), channel_id=1, source_target_pairs={{0,16},{1,17},{2,18},{3,19},{4,20},{5,21},{6,22},{7,23},{8,24},{9,... | collective-permute-start | bytes 294920 | tf_op jit(solution)/shard_map/ppermute | solution.py:10
  75.6 2.6 %collective-permute-done.14 = bf16[128,384]{1,0:T(8,128)(2,1)S(1)} collective-permute-done((bf16[128,384]{1,0:T(8,128)(2,1)S(1)}, bf16[128,384]{1,0:T(8,128)(2,1)S(1)}, u32[]{:S(2)}, u32[]{:S(2)}) %collective-permute-start.14) | collective-permute-done | bytes 98336 | tf_op jit(solution)/shard_map/ppermute | solution.py:10
  78.2 2.2 %fusion = f32[512,384]{1,0:T(8,128)} fusion(f32[512,384]{1,0:T(8,128)S(1)} %fusion.1, bf16[128,384]{1,0:T(8,128)(2,1)S(1)} %collective-permute-done.14, bf16[128,384]{1,0:T(8,128)(2,1)S(1)} %add_convert_fusion, pred[]{:T(512)S(6)} %eq.19, bf16[5,512,128]{2,1,0:T(8,128)(2,1)S(1)} %copy-done.1, bf16[5,128,256]{2,1,0:T(8,128)(2,1)} %param.9), kind=kOutput, calls=%fused_computation.1 | convolution fusion | flops 76627968 | bytes 1966081 | tf_op jit(solution)/shard_map/dot_general | solution.py:39
  (25 shorter events, 2.8 us)
Async XLA Ops:
  0.0 1.0 %copy-start = (bf16[1,512,512]{2,1,0:T(8,128)(2,1)S(1)}, bf16[1,512,512]{2,1,0:T(8,128)(2,1)}, u32[]{:S(2)}) copy-start(bf16[1,512,512]{2,1,0:T(8,128)(2,1)} %param.6) | copy-start | bytes 1572868
  0.0 2.5 %copy-start.2 = (bf16[5,512,128]{2,1,0:T(8,128)(2,1)S(1)}, bf16[5,512,128]{2,1,0:T(8,128)(2,1)}, u32[]{:S(2)}) copy-start(bf16[5,512,128]{2,1,0:T(8,128)(2,1)} %param.7) | copy-start | bytes 1966084
  2.5 1.9 %copy-start.1 = (bf16[5,512,128]{2,1,0:T(8,128)(2,1)S(1)}, bf16[5,512,128]{2,1,0:T(8,128)(2,1)}, u32[]{:S(2)}) copy-start(bf16[5,512,128]{2,1,0:T(8,128)(2,1)} %param.8) | copy-start | bytes 1966084
  2.8 1.6 %collective-permute-start = (bf16[128,384]{1,0:T(8,128)(2,1)S(1)}, bf16[128,384]{1,0:T(8,128)(2,1)}, u32[]{:S(2)}, u32[]{:S(2)}) collective-permute-start(bf16[128,384]{1,0:T(8,128)(2,1)S(1)} %fusion.5), channel_id=1, source_target_pairs={{0,1},{1,0},{2,3},{3,2},{4,5},{5,4},{6,7},{7,6},{8,9},{9,8},{10,11... | collective-permute-start | bytes 294920 | tf_op jit(solution)/shard_map/ppermute | solution.py:10
  6.2 1.5 %collective-permute-start.1 = (f32[128,384]{1,0:T(8,128)S(1)}, f32[128,384]{1,0:T(8,128)S(1)}, u32[]{:S(2)}, u32[]{:S(2)}) collective-permute-start(f32[128,384]{1,0:T(8,128)S(1)} %convolution_bitcast_fusion.8), channel_id=1, source_target_pairs={{0,1},{1,0},{2,3},{3,2},{4,5},{5,4},{6,7},{7,6},{8,9},{9,8},{10,11... | collective-permute-start | bytes 589832 | tf_op jit(solution)/shard_map/ppermute | solution.py:10
  7.7 6.1 %collective-permute-start.2 = (bf16[128,384]{1,0:T(8,128)(2,1)S(1)}, bf16[128,384]{1,0:T(8,128)(2,1)}, u32[]{:S(2)}, u32[]{:S(2)}) collective-permute-start(bf16[128,384]{1,0:T(8,128)(2,1)S(1)} %add_convert_fusion.3), channel_id=1, source_target_pairs={{0,2},{1,3},{2,0},{3,1},{4,6},{5,7},{6,4},{7,5},{8,10},{9,11},{10,... | collective-permute-start | bytes 294920 | tf_op jit(solution)/shard_map/ppermute | solution.py:10
  15.6 1.5 %collective-permute-start.3 = (f32[128,384]{1,0:T(8,128)S(1)}, f32[128,384]{1,0:T(8,128)S(1)}, u32[]{:S(2)}, u32[]{:S(2)}) collective-permute-start(f32[128,384]{1,0:T(8,128)S(1)} %convolution_bitcast_fusion.7), channel_id=1, source_target_pairs={{0,1},{1,0},{2,3},{3,2},{4,5},{5,4},{6,7},{7,6},{8,9},{9,8},{10,11... | collective-permute-start | bytes 589832 | tf_op jit(solution)/shard_map/ppermute | solution.py:10
  17.1 7.0 %collective-permute-start.4 = (f32[128,384]{1,0:T(8,128)S(1)}, f32[128,384]{1,0:T(8,128)S(1)}, u32[]{:S(2)}, u32[]{:S(2)}) collective-permute-start(f32[128,384]{1,0:T(8,128)S(1)} %add.31), channel_id=1, source_target_pairs={{0,2},{1,3},{2,0},{3,1},{4,6},{5,7},{6,4},{7,5},{8,10},{9,11},{10,... | collective-permute-start | bytes 589832 | tf_op jit(solution)/shard_map/ppermute | solution.py:10
  24.2 4.8 %collective-permute-start.5 = (bf16[128,384]{1,0:T(8,128)(2,1)S(1)}, bf16[128,384]{1,0:T(8,128)(2,1)}, u32[]{:S(2)}, u32[]{:S(2)}) collective-permute-start(bf16[128,384]{1,0:T(8,128)(2,1)S(1)} %add_convert_fusion.2), channel_id=1, source_target_pairs={{0,4},{1,5},{2,6},{3,7},{4,0},{5,1},{6,2},{7,3},{8,12},{9,13},{10,... | collective-permute-start | bytes 294920 | tf_op jit(solution)/shard_map/ppermute | solution.py:10
  30.7 1.5 %collective-permute-start.6 = (f32[128,384]{1,0:T(8,128)S(1)}, f32[128,384]{1,0:T(8,128)S(1)}, u32[]{:S(2)}, u32[]{:S(2)}) collective-permute-start(f32[128,384]{1,0:T(8,128)S(1)} %convolution_bitcast_fusion.6), channel_id=1, source_target_pairs={{0,1},{1,0},{2,3},{3,2},{4,5},{5,4},{6,7},{7,6},{8,9},{9,8},{10,11... | collective-permute-start | bytes 589832 | tf_op jit(solution)/shard_map/ppermute | solution.py:10
  32.2 7.0 %collective-permute-start.7 = (f32[128,384]{1,0:T(8,128)S(1)}, f32[128,384]{1,0:T(8,128)S(1)}, u32[]{:S(2)}, u32[]{:S(2)}) collective-permute-start(f32[128,384]{1,0:T(8,128)S(1)} %add.33), channel_id=1, source_target_pairs={{0,2},{1,3},{2,0},{3,1},{4,6},{5,7},{6,4},{7,5},{8,10},{9,11},{10,... | collective-permute-start | bytes 589832 | tf_op jit(solution)/shard_map/ppermute | solution.py:10
  39.3 6.2 %collective-permute-start.8 = (f32[128,384]{1,0:T(8,128)S(1)}, f32[128,384]{1,0:T(8,128)S(1)}, u32[]{:S(2)}, u32[]{:S(2)}) collective-permute-start(f32[128,384]{1,0:T(8,128)S(1)} %add.34), channel_id=1, source_target_pairs={{0,4},{1,5},{2,6},{3,7},{4,0},{5,1},{6,2},{7,3},{8,12},{9,13},{10,... | collective-permute-start | bytes 589832 | tf_op jit(solution)/shard_map/ppermute | solution.py:10
  45.5 4.8 %collective-permute-start.9 = (bf16[128,384]{1,0:T(8,128)(2,1)S(1)}, bf16[128,384]{1,0:T(8,128)(2,1)}, u32[]{:S(2)}, u32[]{:S(2)}) collective-permute-start(bf16[128,384]{1,0:T(8,128)(2,1)S(1)} %add_convert_fusion.1), channel_id=1, source_target_pairs={{0,8},{1,9},{2,10},{3,11},{4,12},{5,13},{6,14},{7,15},{8,0},{9,1},... | collective-permute-start | bytes 294920 | tf_op jit(solution)/shard_map/ppermute | solution.py:10
  52.0 1.5 %collective-permute-start.10 = (f32[128,384]{1,0:T(8,128)S(1)}, f32[128,384]{1,0:T(8,128)S(1)}, u32[]{:S(2)}, u32[]{:S(2)}) collective-permute-start(f32[128,384]{1,0:T(8,128)S(1)} %convolution_bitcast_fusion.5), channel_id=1, source_target_pairs={{0,1},{1,0},{2,3},{3,2},{4,5},{5,4},{6,7},{7,6},{8,9},{9,8},{10,11... | collective-permute-start | bytes 589832 | tf_op jit(solution)/shard_map/ppermute | solution.py:10
  53.6 7.0 %collective-permute-start.11 = (f32[128,384]{1,0:T(8,128)S(1)}, f32[128,384]{1,0:T(8,128)S(1)}, u32[]{:S(2)}, u32[]{:S(2)}) collective-permute-start(f32[128,384]{1,0:T(8,128)S(1)} %add.36), channel_id=1, source_target_pairs={{0,2},{1,3},{2,0},{3,1},{4,6},{5,7},{6,4},{7,5},{8,10},{9,11},{10,... | collective-permute-start | bytes 589832 | tf_op jit(solution)/shard_map/ppermute | solution.py:10
  60.6 6.2 %collective-permute-start.12 = (f32[128,384]{1,0:T(8,128)S(1)}, f32[128,384]{1,0:T(8,128)S(1)}, u32[]{:S(2)}, u32[]{:S(2)}) collective-permute-start(f32[128,384]{1,0:T(8,128)S(1)} %add.37), channel_id=1, source_target_pairs={{0,4},{1,5},{2,6},{3,7},{4,0},{5,1},{6,2},{7,3},{8,12},{9,13},{10,... | collective-permute-start | bytes 589832 | tf_op jit(solution)/shard_map/ppermute | solution.py:10
  66.8 5.7 %collective-permute-start.13 = (f32[128,384]{1,0:T(8,128)S(1)}, f32[128,384]{1,0:T(8,128)S(1)}, u32[]{:S(2)}, u32[]{:S(2)}) collective-permute-start(f32[128,384]{1,0:T(8,128)S(1)} %add.38), channel_id=1, source_target_pairs={{0,8},{1,9},{2,10},{3,11},{4,12},{5,13},{6,14},{7,15},{8,0},{9,1},... | collective-permute-start | bytes 589832 | tf_op jit(solution)/shard_map/ppermute | solution.py:10
  72.5 5.6 %collective-permute-start.14 = (bf16[128,384]{1,0:T(8,128)(2,1)S(1)}, bf16[128,384]{1,0:T(8,128)(2,1)S(1)}, u32[]{:S(2)}, u32[]{:S(2)}) collective-permute-start(bf16[128,384]{1,0:T(8,128)(2,1)S(1)} %add_convert_fusion), channel_id=1, source_target_pairs={{0,16},{1,17},{2,18},{3,19},{4,20},{5,21},{6,22},{7,23},{8,24},{9,... | collective-permute-start | bytes 294920 | tf_op jit(solution)/shard_map/ppermute | solution.py:10
where the time goes:
time: 80.7 us; the launch traced here: 80.4 us
  waiting for transfers between devices  46.4 us (57%)
  starting transfers between devices  21.7 us (27%)
  matrix products  10.9 us (14%)
  local copies, waits for them, and re-layouts  1.05 us (1%)
    ppermute x15, waiting for transfers between devices, partner(): return lax.ppermute(value, axis, pairs)  46.4 us
    ppermute x15, starting transfers between devices, partner(): return lax.ppermute(value, axis, pairs)  21.7 us
    dot_general x5, matrix products, on_device(): jnp.dot(spread_rows[tree_level], coefficients, preferred_element_type=jnp...  8.16 us
  transfers between devices with their start and end apart: 15, of which 15 were waited for; matrix products, arithmetic and copies ran while one was open for 0% of the time, Pallas kernels for 0%

commit v1 on v0

v1 whole, which is shorter than its diff:
```python
import functools

import jax
import jax.numpy as jnp
from jax import lax
from jax.experimental import pallas as pl
from jax.experimental.pallas import tpu as pltpu
from jax.sharding import PartitionSpec as P

MESH = pl.DeviceIdType.MESH
BF16 = jnp.bfloat16
F32 = jnp.float32


def dot_nt(left, right):
    return lax.dot_general(left, right, (((1,), (1,)), ((), ())), preferred_element_type=F32)


def dot_nn(left, right):
    return jnp.dot(left, right, preferred_element_type=F32)


def kernel(
    x_hbm, inv_hbm, p_hbm, s_hbm, c_hbm, o_hbm,
    x, inv, p, s, cap, out, p_t,
    y32, y16, y0r, z32, zs, zr, coef,
    k0s, k0r, kfull, ks, kr, g32, gs, gr,
    load_sem, send_sem, recv_sem,
):
    levels, seg, rank = p.shape
    half = y32.shape[2]
    rhs = 2 * half
    hr = rank // 2
    top = levels - 1
    me = lax.axis_index("seq")
    side = [lax.rem(lax.div(me, 1 << b), 2) for b in range(levels)]
    partner = [me + (1 - 2 * side[b]) * (1 << b) for b in range(levels)]
    core = side[0]
    pairs = [(l, m) for l in range(1, levels) for m in range(l + 1, levels)]
    first = {l: min([i for i, q in enumerate(pairs) if q[0] >= l], default=len(pairs)) for l in range(levels + 1)}
    used = [0]

    def loads(src, dst, i):
        copy = pltpu.make_async_copy(src, dst, load_sem.at[i])
        copy.start()
        return copy

    def send(src, dst, bit):
        i = used[0]
        used[0] += 1
        copy = pltpu.make_async_remote_copy(
            src_ref=src, dst_ref=dst, send_sem=send_sem.at[i], recv_sem=recv_sem.at[i],
            device_id=(partner[bit],), device_id_type=MESH,
        )
        copy.start()
        sent.append(copy)
        return copy

    sent = []
    get_p = loads(p_hbm, p, 0)
    get_s = loads(s_hbm, s, 1)
    get_c = loads(c_hbm, cap, 2)
    get_x = loads(x_hbm, x, 3)
    get_i = loads(inv_hbm.at[0], inv, 4)
    barrier = pltpu.get_barrier_semaphore()
    for b in range(levels):
        pl.semaphore_signal(barrier, inc=1, device_id=(partner[b],), device_id_type=MESH)

    get_p.wait()
    for m in range(1, levels):
        p_t[m] = p[m].T
    get_s.wait()
    get_c.wait()
    for i, (l, m) in enumerate(pairs):
        g = dot_nn(p_t[m], s[l]).reshape(2, hr, rank)
        g32[i] = g
        gs[0, i] = g.astype(BF16)
    for m in range(1, levels):
        k0s[m - 1] = dot_nn(dot_nn(p_t[m], s[0]).astype(BF16), cap[0]).astype(BF16)
    pl.semaphore_wait(barrier, levels)
    g_copy = {}
    k_copy = {}
    z_copy = {}
    c_copy = {}
    if pairs:
        g_copy[0] = send(gs.at[0, :, 1 - core], gr.at[0], 0)
    k_copy[0] = send(k0s, k0r, 0)

    get_x.wait()
    x_t = x[...].T
    get_i.wait()
    st = dot_nt(x_t, inv[...]).astype(BF16)
    for m in range(levels):
        y = dot_nn(st, p[m]).reshape(2, half, rank)
        y16[m] = y.astype(BF16)
        if m == 0:
            z_copy[0, 0] = send(y16.at[0], y0r, 0)
        else:
            y32[m] = y
    z_copy[0, 1] = send(y16.at[pl.ds(1, top), 1 - core], zr.at[0, pl.ds(1, top)], 0)

    def g_step(b):
        lo = first[b + 1]
        if lo >= len(pairs):
            return
        g_copy[b].wait_recv()
        for i in range(lo, len(pairs)):
            old = g32[i, core] if b == 0 else g32[i, 0]
            g = old + gr[b, i].astype(F32)
            g32[i, 0] = g
            if pairs[i][0] == b + 1:
                j = pairs[i][1] - (b + 2)
                kp = dot_nn(g.astype(BF16), cap[b + 1])
                ks[b + 1, j] = kp.astype(BF16)
            else:
                gs[b + 1, i, 0] = g.astype(BF16)
        n = top - (b + 1)
        k_copy[b + 1] = send(ks.at[b + 1, pl.ds(0, n)], kr.at[b + 1, pl.ds(0, n)], b + 1)
        nxt = first[b + 2]
        if nxt < len(pairs):
            rest = pl.ds(nxt, len(pairs) - nxt)
            g_copy[b + 1] = send(gs.at[b + 1, rest, 0], gr.at[b + 1, rest], b + 1)

    def k_sum(l):
        n = top - l
        k_copy[l].wait_recv()
        for j in range(n):
            kfull[l, j, core] = (ks[l, j].astype(F32) + kr[l, j].astype(F32)).astype(BF16)
        mine = kfull.at[l, pl.ds(0, n), core]
        return send(mine, mine, 0)

    def stack(own, other, l):
        low = side[l] == 0
        return jnp.concatenate([jnp.where(low, own, other), jnp.where(low, other, own)], 1)

    g_step(0)
    out[...] = dot_nn(inv[...], x[...])

    k_copy[0].wait_recv()
    for j in range(top):
        kfull[0, j] = (k0s[j].astype(F32) + k0r[j].astype(F32)).astype(BF16).reshape(2, hr, 2 * rank)
    z_copy[0, 0].wait_recv()
    stacked = stack(y16[0, core], y0r[core], 0)
    z_copy[0, 1].wait_recv()
    for m in range(1, levels):
        z = y32[m, core] + zr[0, m].astype(F32) - dot_nt(stacked, kfull[0, m - 1].reshape(rank, 2 * rank))
        z32[m] = z
        zs[1, m] = z.astype(BF16)
        z_copy[1, m] = send(zs.at[1, m], zr.at[1, m], 1)
    g_step(1)
    stacked = stack(y16[0].reshape(rhs, rank), y0r[...].reshape(rhs, rank), 0)
    coef[0] = dot_nt(stacked, cap[0]).astype(BF16).reshape(2, half, rank)
    out[...] -= dot_nt(s[0], coef[0].reshape(rhs, rank))

    for l in range(1, levels):
        if l < top:
            k_done = k_sum(l)
        z_copy[l, l].wait_recv()
        stacked = stack(zs[l, l], zr[l, l], l)
        coef[l, core] = dot_nt(stacked, cap[l]).astype(BF16)
        c_copy[l] = send(coef.at[l, core], coef.at[l, core], 0)
        if l < top:
            k_done.wait_recv()
            for m in range(l + 1, levels):
                z_copy[l, m].wait_recv()
                z = z32[m] + zr[l, m].astype(F32) - dot_nt(stacked, kfull[l, m - l - 1].reshape(rank, 2 * rank))
                z32[m] = z
                zs[l + 1, m] = z.astype(BF16)
                z_copy[l + 1, m] = send(zs.at[l + 1, m], zr.at[l + 1, m], l + 1)
            g_step(l + 1)
            c_copy[l].wait_recv()
            out[...] -= dot_nt(s[l], coef[l].reshape(rhs, rank))
    c_copy[top].wait_recv()
    c_last = coef[top].reshape(rhs, rank)
    pieces = 4
    rows = seg // pieces
    puts = []
    for i in range(pieces):
        part = pl.ds(i * rows, rows)
        out[part] = out[part] - dot_nt(s[top, part], c_last)
        puts.append(loads(out.at[part], o_hbm.at[part], 5 + i))
    for copy in sent:
        copy.wait_send()
    for put in puts:
        put.wait()


def on_device(right_side, leaf_inverse, project_rows, spread_rows, capacity):
    levels, seg, rank = project_rows.shape
    rhs = right_side.shape[1]
    half = rhs // 2
    hr = rank // 2
    pairs = max(1, (levels - 1) * (levels - 2) // 2)
    copies = levels * levels + 6 * levels
    vmem = pltpu.VMEM
    return pl.pallas_call(
        kernel,
        name="hodlr_solve",
        out_shape=jax.ShapeDtypeStruct((seg, rhs), F32),
        in_specs=[pl.BlockSpec(memory_space=pl.ANY)] * 5,
        out_specs=pl.BlockSpec(memory_space=pl.ANY),
        scratch_shapes=[
            vmem((seg, rhs), BF16),
            vmem((seg, seg), BF16),
            vmem((levels, seg, rank), BF16),
            vmem((levels, seg, rank), BF16),
            vmem((levels, rank, 2 * rank), BF16),
            vmem((seg, rhs), F32),
            vmem((levels, rank, seg), BF16),
            vmem((levels, 2, half, rank), F32),
            vmem((levels, 2, half, rank), BF16),
            vmem((2, half, rank), BF16),
            vmem((levels, half, rank), F32),
            vmem((levels, levels, half, rank), BF16),
            vmem((levels, levels, half, rank), BF16),
            vmem((levels, 2, half, rank), BF16),
            vmem((levels - 1, rank, 2 * rank), BF16),
            vmem((levels - 1, rank, 2 * rank), BF16),
            vmem((levels - 1, levels - 1, 2, hr, 2 * rank), BF16),
            vmem((levels - 1, levels - 1, hr, 2 * rank), BF16),
            vmem((levels - 1, levels - 1, hr, 2 * rank), BF16),
            vmem((pairs, 2, hr, rank), F32),
            vmem((levels - 1, pairs, 2, hr, rank), BF16),
            vmem((levels - 1, pairs, hr, rank), BF16),
            pltpu.SemaphoreType.DMA((9,)),
            pltpu.SemaphoreType.DMA((copies,)),
            pltpu.SemaphoreType.DMA((copies,)),
        ],
        compiler_params=pltpu.CompilerParams(
            collective_id=0, has_side_effects=True, vmem_limit_bytes=56 * 2**20
        ),
    )(right_side, leaf_inverse, project_rows, spread_rows, capacity)


def solution(mesh):
    return jax.shard_map(
        on_device,
        mesh=mesh,
        in_specs=(
            P("seq", None),
            P("seq", None, None),
            P(None, "seq", None),
            P(None, "seq", None),
            P(None, "seq", None),
        ),
        out_specs=P("seq", None),
        check_vma=False,
    )
```

time: 80.7 us -> 33.7 us (0.42)
  the two profiles are of different devices: /device:TPU:0 before, /device:TPU:1 now
where the time goes in v1:
time: 33.7 us; the launch traced here: 33.5 us
  Pallas kernels  31.4 us (93%)
  local copies, waits for them, and re-layouts  2.06 us (6%)
    pallas_call x1, Pallas kernels, on_device(): pl.pallas_call(kernel, name='hodlr_solve', out_shape=jax.ShapeDtypeStruct...  31.4 us
    unnamed x1, local copies, waits for them, and re-layouts  2.06 us

profile of v1, /device:TPU:1, one launch (start us, length us, event | category | flops | bytes accessed | tf_op | source)
XLA Modules:
  0.0 33.5 jit_solution(15070600857585602590)
XLA Ops:
  0.0 31.4 %hodlr_solve.1 = f32[512,384]{1,0:T(8,128)} custom-call(bf16[512,384]{1,0:T(8,128)(2,1)} %x_hbm.1, bf16[1,512,512]{2,1,0:T(8,128)(2,1)} %inv_hbm.1, bf16[5,512,128]{2,1,0:T(8,128)(2,1)} %p_hbm.1, bf16[5,512,128]{2,1,0:T(8,128)(2,1)} %s_hbm.1, bf16[5,128,256]{2,1,0:T(8,128)(2,1)} %c_hbm.1), custom_call_target="tpu_custom_call" | custom-call | tf_op jit(solution)/shard_map/hodlr_solve/pallas_call | solution.py:196
  31.5 2.1 %copy.7 = f32[512,384]{1,0:T(8,128)} copy(f32[512,384]{1,0:T(8,128)} %hodlr_solve.1) | data formatting | bytes 1572864

commit v2 on v1

--- a/solution.py
+++ b/solution.py
@@ -21,8 +21,8 @@
 
 
 def kernel(
-    x_hbm, inv_hbm, p_hbm, s_hbm, c_hbm, o_hbm,
-    x, inv, p, s, cap, out, p_t,
+    x_hbm, inv_hbm, p_hbm, s_hbm, c_hbm, out,
+    x, inv, p, s, cap, p_t,
     y32, y16, y0r, z32, zs, zr, coef,
     k0s, k0r, kfull, ks, kr, g32, gs, gr,
     load_sem, send_sem, recv_sem,
@@ -172,17 +172,9 @@
             out[...] -= dot_nt(s[l], coef[l].reshape(rhs, rank))
     c_copy[top].wait_recv()
     c_last = coef[top].reshape(rhs, rank)
-    pieces = 4
-    rows = seg // pieces
-    puts = []
-    for i in range(pieces):
-        part = pl.ds(i * rows, rows)
-        out[part] = out[part] - dot_nt(s[top, part], c_last)
-        puts.append(loads(out.at[part], o_hbm.at[part], 5 + i))
+    out[...] -= dot_nt(s[top], c_last)
     for copy in sent:
         copy.wait_send()
-    for put in puts:
-        put.wait()
 
 
 def on_device(right_side, leaf_inverse, project_rows, spread_rows, capacity):
@@ -196,16 +188,15 @@
     return pl.pallas_call(
         kernel,
         name="hodlr_solve",
-        out_shape=jax.ShapeDtypeStruct((seg, rhs), F32),
-        in_specs=[pl.BlockSpec(memory_space=pl.ANY)] * 5,
-        out_specs=pl.BlockSpec(memory_space=pl.ANY),
+        out_shape=pltpu.VMEM((seg, rhs), F32),
+        in_specs=[pl.BlockSpec(memory_space=pltpu.HBM)] * 5,
+        out_specs=pl.BlockSpec(memory_space=pltpu.VMEM),
         scratch_shapes=[
             vmem((seg, rhs), BF16),
             vmem((seg, seg), BF16),
             vmem((levels, seg, rank), BF16),
             vmem((levels, seg, rank), BF16),
             vmem((levels, rank, 2 * rank), BF16),
-            vmem((seg, rhs), F32),
             vmem((levels, rank, seg), BF16),
             vmem((levels, 2, half, rank), F32),
             vmem((levels, 2, half, rank), BF16),
@@ -222,7 +213,7 @@
             vmem((pairs, 2, hr, rank), F32),
             vmem((levels - 1, pairs, 2, hr, rank), BF16),
             vmem((levels - 1, pairs, hr, rank), BF16),
-            pltpu.SemaphoreType.DMA((9,)),
+            pltpu.SemaphoreType.DMA((5,)),
             pltpu.SemaphoreType.DMA((copies,)),
             pltpu.SemaphoreType.DMA((copies,)),
         ],

time: 33.7 us -> 31.7 us (0.941)
  the two profiles are of different devices: /device:TPU:1 before, /device:TPU:0 now
where the time goes in v2:
time: 31.7 us; the launch traced here: 31.4 us
  Pallas kernels  30.5 us (96%)
  local copies, waits for them, and re-layouts  0.88 us (3%)
    pallas_call x1, Pallas kernels, on_device(): pl.pallas_call(kernel, name='hodlr_solve', out_shape=pltpu.VMEM((seg, rhs...  30.5 us
    unnamed x1, local copies, waits for them, and re-layouts  0.88 us

profile of v2, /device:TPU:0, one launch (start us, length us, event | category | flops | bytes accessed | tf_op | source)
XLA Modules:
  0.0 31.4 jit_solution(17430553475446377351)
XLA Ops:
  0.0 30.5 %hodlr_solve.1 = f32[512,384]{1,0:T(8,128)S(1)} custom-call(bf16[512,384]{1,0:T(8,128)(2,1)} %x_hbm.1, bf16[1,512,512]{2,1,0:T(8,128)(2,1)} %inv_hbm.1, bf16[5,512,128]{2,1,0:T(8,128)(2,1)} %p_hbm.1, bf16[5,512,128]{2,1,0:T(8,128)(2,1)} %s_hbm.1, bf16[5,128,256]{2,1,0:T(8,128)(2,1)} %c_hbm.1), custom_call_target="tpu_custom_call" | custom-call | tf_op jit(solution)/shard_map/hodlr_solve/pallas_call | solution.py:188
  30.5 0.9 %copy.7 = f32[512,384]{1,0:T(8,128)} copy(f32[512,384]{1,0:T(8,128)S(1)} %hodlr_solve.1) | data formatting | bytes 1572864

commit v3 on v2

--- a/solution.py
+++ b/solution.py
@@ -23,12 +23,13 @@
 def kernel(
     x_hbm, inv_hbm, p_hbm, s_hbm, c_hbm, out,
     x, inv, p, s, cap, p_t,
-    y32, y16, y0r, z32, zs, zr, coef,
-    k0s, k0r, kfull, ks, kr, g32, gs, gr,
+    y32, y16, y0r, zr0, z1s, z1r, zb32, zb16, zbr, z32, zs, zr, coef,
+    g1f, g1s, g1r, k0s, k0r, kfull, ks, kr, g32, gs, gr,
     load_sem, send_sem, recv_sem,
 ):
     levels, seg, rank = p.shape
     half = y32.shape[2]
+    quarter = half // 2
     rhs = 2 * half
     hr = rank // 2
     top = levels - 1
@@ -36,7 +37,9 @@
     side = [lax.rem(lax.div(me, 1 << b), 2) for b in range(levels)]
     partner = [me + (1 - 2 * side[b]) * (1 << b) for b in range(levels)]
     core = side[0]
-    pairs = [(l, m) for l in range(1, levels) for m in range(l + 1, levels)]
+    xside = side[1]
+    diagonal = partner[1] + partner[0] - me
+    pairs = [(l, m) for l in range(2, levels) for m in range(l + 1, levels)]
     first = {l: min([i for i, q in enumerate(pairs) if q[0] >= l], default=len(pairs)) for l in range(levels + 1)}
     used = [0]
 
@@ -45,12 +48,12 @@
         copy.start()
         return copy
 
-    def send(src, dst, bit):
+    def send(src, dst, bit, target=None):
         i = used[0]
         used[0] += 1
         copy = pltpu.make_async_remote_copy(
             src_ref=src, dst_ref=dst, send_sem=send_sem.at[i], recv_sem=recv_sem.at[i],
-            device_id=(partner[bit],), device_id_type=MESH,
+            device_id=(partner[bit] if target is None else target,), device_id_type=MESH,
         )
         copy.start()
         sent.append(copy)
@@ -65,25 +68,32 @@
     barrier = pltpu.get_barrier_semaphore()
     for b in range(levels):
         pl.semaphore_signal(barrier, inc=1, device_id=(partner[b],), device_id_type=MESH)
+    pl.semaphore_signal(barrier, inc=1, device_id=(diagonal,), device_id_type=MESH)
 
     get_p.wait()
     for m in range(1, levels):
         p_t[m] = p[m].T
     get_s.wait()
     get_c.wait()
-    for i, (l, m) in enumerate(pairs):
-        g = dot_nn(p_t[m], s[l]).reshape(2, hr, rank)
-        g32[i] = g
-        gs[0, i] = g.astype(BF16)
-    for m in range(1, levels):
-        k0s[m - 1] = dot_nn(dot_nn(p_t[m], s[0]).astype(BF16), cap[0]).astype(BF16)
-    pl.semaphore_wait(barrier, levels)
+    for l in range(1, levels - 1):
+        products = dot_nn(p_t[l + 1 : levels].reshape((top - l) * rank, seg), s[l])
+        if l == 1:
+            g1f[...] = products
+            g1s[...] = products.astype(BF16)
+        else:
+            products = products.reshape(top - l, 2, hr, rank)
+            g32[first[l] : first[l] + top - l] = products
+            gs[0, first[l] : first[l] + top - l] = products.astype(BF16)
+    products = dot_nn(p_t[1:levels].reshape(top * rank, seg), s[0]).astype(BF16)
+    k0s[...] = dot_nn(products, cap[0]).astype(BF16)
+    pl.semaphore_wait(barrier, levels + 1)
     g_copy = {}
     k_copy = {}
     z_copy = {}
     c_copy = {}
     if pairs:
         g_copy[0] = send(gs.at[0, :, 1 - core], gr.at[0], 0)
+    g1_copy = send(g1s, g1r, 0)
     k_copy[0] = send(k0s, k0r, 0)
 
     get_x.wait()
@@ -97,7 +107,7 @@
             z_copy[0, 0] = send(y16.at[0], y0r, 0)
         else:
             y32[m] = y
-    z_copy[0, 1] = send(y16.at[pl.ds(1, top), 1 - core], zr.at[0, pl.ds(1, top)], 0)
+    z_copy[0, 1] = send(y16.at[pl.ds(1, top), 1 - core], zr0.at[pl.ds(1, top)], 0)
 
     def g_step(b):
         lo = first[b + 1]
@@ -114,8 +124,9 @@
                 ks[b + 1, j] = kp.astype(BF16)
             else:
                 gs[b + 1, i, 0] = g.astype(BF16)
-        n = top - (b + 1)
-        k_copy[b + 1] = send(ks.at[b + 1, pl.ds(0, n)], kr.at[b + 1, pl.ds(0, n)], b + 1)
+        if b >= 1:
+            n = top - (b + 1)
+            k_copy[b + 1] = send(ks.at[b + 1, pl.ds(0, n)], kr.at[b + 1, pl.ds(0, n)], b + 1)
         nxt = first[b + 2]
         if nxt < len(pairs):
             rest = pl.ds(nxt, len(pairs) - nxt)
@@ -134,31 +145,52 @@
         return jnp.concatenate([jnp.where(low, own, other), jnp.where(low, other, own)], 1)
 
     g_step(0)
-    out[...] = dot_nn(inv[...], x[...])
 
     k_copy[0].wait_recv()
-    for j in range(top):
-        kfull[0, j] = (k0s[j].astype(F32) + k0r[j].astype(F32)).astype(BF16).reshape(2, hr, 2 * rank)
+    k0r[...] = (k0s[...].astype(F32) + k0r[...].astype(F32)).astype(BF16)
     z_copy[0, 0].wait_recv()
     stacked = stack(y16[0, core], y0r[core], 0)
     z_copy[0, 1].wait_recv()
     for m in range(1, levels):
-        z = y32[m, core] + zr[0, m].astype(F32) - dot_nt(stacked, kfull[0, m - 1].reshape(rank, 2 * rank))
+        z = y32[m, core] + zr0[m].astype(F32) - dot_nt(stacked, k0r[(m - 1) * rank : m * rank])
+        if m == 1:
+            z1s[...] = z.astype(BF16)
+            z_copy[1, 1] = send(z1s, z1r, 1)
+        else:
+            zb32[m] = z.reshape(2, quarter, rank)
+    g1_copy.wait_recv()
+    g1s_sum = (g1f[...] + g1r[...].astype(F32)).astype(BF16)
+    g1f[...] = g1s_sum.astype(F32)
+    g_step(1)
+    out[...] = dot_nn(inv[...], x[...])
+    stacked = stack(y16[0].reshape(rhs, rank), y0r[...].reshape(rhs, rank), 0)
+    coef[0] = dot_nt(stacked, cap[0]).astype(BF16).reshape(2, 2, quarter, rank)
+    out[...] -= dot_nt(s[0], coef[0].reshape(rhs, rank))
+
+    z_copy[1, 1].wait_recv()
+    c_one = dot_nt(stack(z1s[...], z1r[...], 1), cap[1]).astype(BF16)
+    coef[1, core] = c_one.reshape(2, quarter, rank)
+    for m in range(2, levels):
+        g = g1f[(m - 2) * rank : (m - 1) * rank].astype(BF16)
+        z = zb32[m] - dot_nt(c_one, g).reshape(2, quarter, rank)
+        zb32[m] = z
+        zb16[m] = z.astype(BF16)
+        z_copy[1, m] = send(zb16.at[m, 1 - xside], zbr.at[m], 1)
+    c_copy[1] = send(coef.at[1, core], coef.at[1, core], 0)
+    k_done = k_sum(2)
+    c_copy[1].wait_recv()
+    out[...] -= dot_nt(s[1], coef[1].reshape(rhs, rank))
+    for m in range(2, levels):
+        z_copy[1, m].wait_recv()
+        z = zb32[m, xside] + zbr[m].astype(F32)
         z32[m] = z
-        zs[1, m] = z.astype(BF16)
-        z_copy[1, m] = send(zs.at[1, m], zr.at[1, m], 1)
-    g_step(1)
-    stacked = stack(y16[0].reshape(rhs, rank), y0r[...].reshape(rhs, rank), 0)
-    coef[0] = dot_nt(stacked, cap[0]).astype(BF16).reshape(2, half, rank)
-    out[...] -= dot_nt(s[0], coef[0].reshape(rhs, rank))
-
-    for l in range(1, levels):
-        if l < top:
-            k_done = k_sum(l)
+        zs[2, m] = z.astype(BF16)
+        z_copy[2, m] = send(zs.at[2, m], zr.at[2, m], 2)
+    g_step(2)
+
+    for l in range(2, levels):
         z_copy[l, l].wait_recv()
         stacked = stack(zs[l, l], zr[l, l], l)
-        coef[l, core] = dot_nt(stacked, cap[l]).astype(BF16)
-        c_copy[l] = send(coef.at[l, core], coef.at[l, core], 0)
         if l < top:
             k_done.wait_recv()
             for m in range(l + 1, levels):
@@ -167,10 +199,18 @@
                 z32[m] = z
                 zs[l + 1, m] = z.astype(BF16)
                 z_copy[l + 1, m] = send(zs.at[l + 1, m], zr.at[l + 1, m], l + 1)
-            g_step(l + 1)
-            c_copy[l].wait_recv()
+        coef[l, core, xside] = dot_nt(stacked, cap[l]).astype(BF16)
+        mine = coef.at[l, core, xside]
+        c_copy[l] = [send(mine, mine, 1, diagonal), send(mine, mine, 1), send(mine, mine, 0)]
+        if l < top:
+            if l + 1 < top:
+                g_step(l + 1)
+                k_done = k_sum(l + 1)
+            for copy in c_copy[l]:
+                copy.wait_recv()
             out[...] -= dot_nt(s[l], coef[l].reshape(rhs, rank))
-    c_copy[top].wait_recv()
+    for copy in c_copy[top]:
+        copy.wait_recv()
     c_last = coef[top].reshape(rhs, rank)
     out[...] -= dot_nt(s[top], c_last)
     for copy in sent:
@@ -181,8 +221,9 @@
     levels, seg, rank = project_rows.shape
     rhs = right_side.shape[1]
     half = rhs // 2
+    quarter = half // 2
     hr = rank // 2
-    pairs = max(1, (levels - 1) * (levels - 2) // 2)
+    pairs = max(1, (levels - 2) * (levels - 3) // 2)
     copies = levels * levels + 6 * levels
     vmem = pltpu.VMEM
     return pl.pallas_call(
@@ -201,12 +242,21 @@
             vmem((levels, 2, half, rank), F32),
             vmem((levels, 2, half, rank), BF16),
             vmem((2, half, rank), BF16),
-            vmem((levels, half, rank), F32),
-            vmem((levels, levels, half, rank), BF16),
-            vmem((levels, levels, half, rank), BF16),
-            vmem((levels, 2, half, rank), BF16),
-            vmem((levels - 1, rank, 2 * rank), BF16),
-            vmem((levels - 1, rank, 2 * rank), BF16),
+            vmem((levels, half, rank), BF16),
+            vmem((half, rank), BF16),
+            vmem((half, rank), BF16),
+            vmem((levels, 2, quarter, rank), F32),
+            vmem((levels, 2, quarter, rank), BF16),
+            vmem((levels, quarter, rank), BF16),
+            vmem((levels, quarter, rank), F32),
+            vmem((levels, levels, quarter, rank), BF16),
+            vmem((levels, levels, quarter, rank), BF16),
+            vmem((levels, 2, 2, quarter, rank), BF16),
+            vmem(((levels - 2) * rank, rank), F32),
+            vmem(((levels - 2) * rank, rank), BF16),
+            vmem(((levels - 2) * rank, rank), BF16),
+            vmem(((levels - 1) * rank, 2 * rank), BF16),
+            vmem(((levels - 1) * rank, 2 * rank), BF16),
             vmem((levels - 1, levels - 1, 2, hr, 2 * rank), BF16),
             vmem((levels - 1, levels - 1, hr, 2 * rank), BF16),
             vmem((levels - 1, levels - 1, hr, 2 * rank), BF16),

time: 31.7 us -> 31 us (0.978)
  Pallas kernels: 30.5 us -> 29.9 us
    pallas_call x1, Pallas kernels: 30.5 us -> 29.9 us  [on_device(): pl.pallas_call(kernel, name='hodlr_solve', out_shape=pltpu.VMEM((seg, rhs...]
where the time goes in v3:
time: 31 us; the launch traced here: 30.8 us
  Pallas kernels  29.9 us (96%)
  local copies, waits for them, and re-layouts  0.88 us (3%)
    pallas_call x1, Pallas kernels, on_device(): pl.pallas_call(kernel, name='hodlr_solve', out_shape=pltpu.VMEM((seg, rhs...  29.9 us
    unnamed x1, local copies, waits for them, and re-layouts  0.88 us

profile of v3, /device:TPU:0, one launch (start us, length us, event | category | flops | bytes accessed | tf_op | source)
XLA Modules:
  0.0 30.8 jit_solution(15128208021642018899)
XLA Ops:
  0.0 29.9 %hodlr_solve.1 = f32[512,384]{1,0:T(8,128)S(1)} custom-call(bf16[512,384]{1,0:T(8,128)(2,1)} %x_hbm.1, bf16[1,512,512]{2,1,0:T(8,128)(2,1)} %inv_hbm.1, bf16[5,512,128]{2,1,0:T(8,128)(2,1)} %p_hbm.1, bf16[5,512,128]{2,1,0:T(8,128)(2,1)} %s_hbm.1, bf16[5,128,256]{2,1,0:T(8,128)(2,1)} %c_hbm.1), custom_call_target="tpu_custom_call" | custom-call | tf_op jit(solution)/shard_map/hodlr_solve/pallas_call | solution.py:229
  29.9 0.9 %copy.7 = f32[512,384]{1,0:T(8,128)} copy(f32[512,384]{1,0:T(8,128)S(1)} %hodlr_solve.1) | data formatting | bytes 1572864

commit v4 on v3

--- a/solution.py
+++ b/solution.py
@@ -60,54 +60,54 @@
         return copy
 
     sent = []
-    get_p = loads(p_hbm, p, 0)
-    get_s = loads(s_hbm, s, 1)
-    get_c = loads(c_hbm, cap, 2)
-    get_x = loads(x_hbm, x, 3)
-    get_i = loads(inv_hbm.at[0], inv, 4)
+    get_x = loads(x_hbm, x, 0)
+    get_i = loads(inv_hbm.at[0], inv, 1)
+    get_p = loads(p_hbm, p, 2)
+    get_s = loads(s_hbm, s, 3)
+    get_c = loads(c_hbm, cap, 4)
     barrier = pltpu.get_barrier_semaphore()
     for b in range(levels):
         pl.semaphore_signal(barrier, inc=1, device_id=(partner[b],), device_id_type=MESH)
     pl.semaphore_signal(barrier, inc=1, device_id=(diagonal,), device_id_type=MESH)
 
+    g_copy = {}
+    k_copy = {}
+    z_copy = {}
+    c_copy = {}
+
+    get_x.wait()
+    x_t = x[...].T
+    get_i.wait()
+    st = dot_nt(x_t, inv[...]).astype(BF16)
     get_p.wait()
+    for m in range(levels):
+        y = dot_nn(st, p[m]).reshape(2, half, rank)
+        y16[m] = y.astype(BF16)
+        if m > 0:
+            y32[m] = y
+    pl.semaphore_wait(barrier, levels + 1)
+    z_copy[0, 0] = send(y16.at[0], y0r, 0)
+    z_copy[0, 1] = send(y16.at[pl.ds(1, top), 1 - core], zr0.at[pl.ds(1, top)], 0)
+
     for m in range(1, levels):
         p_t[m] = p[m].T
     get_s.wait()
     get_c.wait()
-    for l in range(1, levels - 1):
+    products = dot_nn(p_t[1:levels].reshape(top * rank, seg), s[0]).astype(BF16)
+    k0s[...] = dot_nn(products, cap[0]).astype(BF16)
+    k_copy[0] = send(k0s, k0r, 0)
+    for l in range(levels - 2, 0, -1):
         products = dot_nn(p_t[l + 1 : levels].reshape((top - l) * rank, seg), s[l])
         if l == 1:
             g1f[...] = products
             g1s[...] = products.astype(BF16)
+            g1_copy = send(g1s, g1r, 0)
         else:
             products = products.reshape(top - l, 2, hr, rank)
             g32[first[l] : first[l] + top - l] = products
             gs[0, first[l] : first[l] + top - l] = products.astype(BF16)
-    products = dot_nn(p_t[1:levels].reshape(top * rank, seg), s[0]).astype(BF16)
-    k0s[...] = dot_nn(products, cap[0]).astype(BF16)
-    pl.semaphore_wait(barrier, levels + 1)
-    g_copy = {}
-    k_copy = {}
-    z_copy = {}
-    c_copy = {}
-    if pairs:
-        g_copy[0] = send(gs.at[0, :, 1 - core], gr.at[0], 0)
-    g1_copy = send(g1s, g1r, 0)
-    k_copy[0] = send(k0s, k0r, 0)
-
-    get_x.wait()
-    x_t = x[...].T
-    get_i.wait()
-    st = dot_nt(x_t, inv[...]).astype(BF16)
-    for m in range(levels):
-        y = dot_nn(st, p[m]).reshape(2, half, rank)
-        y16[m] = y.astype(BF16)
-        if m == 0:
-            z_copy[0, 0] = send(y16.at[0], y0r, 0)
-        else:
-            y32[m] = y
-    z_copy[0, 1] = send(y16.at[pl.ds(1, top), 1 - core], zr0.at[pl.ds(1, top)], 0)
+            if l == 2:
+                g_copy[0] = send(gs.at[0, :, 1 - core], gr.at[0], 0)
 
     def g_step(b):
         lo = first[b + 1]
@@ -144,8 +144,6 @@
         low = side[l] == 0
         return jnp.concatenate([jnp.where(low, own, other), jnp.where(low, other, own)], 1)
 
-    g_step(0)
-
     k_copy[0].wait_recv()
     k0r[...] = (k0s[...].astype(F32) + k0r[...].astype(F32)).astype(BF16)
     z_copy[0, 0].wait_recv()
@@ -158,10 +156,10 @@
             z_copy[1, 1] = send(z1s, z1r, 1)
         else:
             zb32[m] = z.reshape(2, quarter, rank)
+    g_step(0)
     g1_copy.wait_recv()
     g1s_sum = (g1f[...] + g1r[...].astype(F32)).astype(BF16)
     g1f[...] = g1s_sum.astype(F32)
-    g_step(1)
     out[...] = dot_nn(inv[...], x[...])
     stacked = stack(y16[0].reshape(rhs, rank), y0r[...].reshape(rhs, rank), 0)
     coef[0] = dot_nt(stacked, cap[0]).astype(BF16).reshape(2, 2, quarter, rank)
@@ -177,16 +175,17 @@
         zb16[m] = z.astype(BF16)
         z_copy[1, m] = send(zb16.at[m, 1 - xside], zbr.at[m], 1)
     c_copy[1] = send(coef.at[1, core], coef.at[1, core], 0)
-    k_done = k_sum(2)
-    c_copy[1].wait_recv()
-    out[...] -= dot_nt(s[1], coef[1].reshape(rhs, rank))
+    g_step(1)
     for m in range(2, levels):
         z_copy[1, m].wait_recv()
         z = zb32[m, xside] + zbr[m].astype(F32)
         z32[m] = z
         zs[2, m] = z.astype(BF16)
         z_copy[2, m] = send(zs.at[2, m], zr.at[2, m], 2)
+    k_done = k_sum(2)
     g_step(2)
+    c_copy[1].wait_recv()
+    out[...] -= dot_nt(s[1], coef[1].reshape(rhs, rank))
 
     for l in range(2, levels):
         z_copy[l, l].wait_recv()
@@ -204,17 +203,17 @@
         c_copy[l] = [send(mine, mine, 1, diagonal), send(mine, mine, 1), send(mine, mine, 0)]
         if l < top:
             if l + 1 < top:
+                k_done = k_sum(l + 1)
                 g_step(l + 1)
-                k_done = k_sum(l + 1)
-            for copy in c_copy[l]:
-                copy.wait_recv()
+    for l in range(2, levels):
+        for copy in c_copy[l]:
+            copy.wait_recv()
+        if l < top:
             out[...] -= dot_nt(s[l], coef[l].reshape(rhs, rank))
-    for copy in c_copy[top]:
-        copy.wait_recv()
+    for copy in sent:
+        copy.wait_send()
     c_last = coef[top].reshape(rhs, rank)
     out[...] -= dot_nt(s[top], c_last)
-    for copy in sent:
-        copy.wait_send()
 
 
 def on_device(right_side, leaf_inverse, project_rows, spread_rows, capacity):

time: 31 us -> 30.8 us (level)
  no operation moved by 1% of the time
where the time goes in v4:
time: 30.8 us; the launch traced here: 30.7 us
  Pallas kernels  29.8 us (97%)
  local copies, waits for them, and re-layouts  0.88 us (3%)
    pallas_call x1, Pallas kernels, on_device(): pl.pallas_call(kernel, name='hodlr_solve', out_shape=pltpu.VMEM((seg, rhs...  29.8 us
    unnamed x1, local copies, waits for them, and re-layouts  0.88 us

profile of v4, /device:TPU:0, one launch (start us, length us, event | category | flops | bytes accessed | tf_op | source)
XLA Modules:
  0.0 30.7 jit_solution(11549330537818441210)
XLA Ops:
  0.0 29.8 %hodlr_solve.1 = f32[512,384]{1,0:T(8,128)S(1)} custom-call(bf16[512,384]{1,0:T(8,128)(2,1)} %x_hbm.1, bf16[1,512,512]{2,1,0:T(8,128)(2,1)} %inv_hbm.1, bf16[5,512,128]{2,1,0:T(8,128)(2,1)} %p_hbm.1, bf16[5,512,128]{2,1,0:T(8,128)(2,1)} %s_hbm.1, bf16[5,128,256]{2,1,0:T(8,128)(2,1)} %c_hbm.1), custom_call_target="tpu_custom_call" | custom-call | tf_op jit(solution)/shard_map/hodlr_solve/pallas_call | solution.py:228
  29.8 0.9 %copy.7 = f32[512,384]{1,0:T(8,128)} copy(f32[512,384]{1,0:T(8,128)S(1)} %hodlr_solve.1) | data formatting | bytes 1572864

commit v5 on v4

--- a/solution.py
+++ b/solution.py
@@ -51,20 +51,31 @@
     def send(src, dst, bit, target=None):
         i = used[0]
         used[0] += 1
+        out_i = free.pop(0)
         copy = pltpu.make_async_remote_copy(
-            src_ref=src, dst_ref=dst, send_sem=send_sem.at[i], recv_sem=recv_sem.at[i],
+            src_ref=src, dst_ref=dst, send_sem=send_sem.at[out_i], recv_sem=recv_sem.at[i],
             device_id=(partner[bit] if target is None else target,), device_id_type=MESH,
         )
         copy.start()
-        sent.append(copy)
+        sent.append((copy, out_i))
         return copy
 
+    def reap(count):
+        while len(sent) > count:
+            copy, i = sent.pop(0)
+            copy.wait_send()
+            free.append(i)
+
     sent = []
-    get_x = loads(x_hbm, x, 0)
-    get_i = loads(inv_hbm.at[0], inv, 1)
-    get_p = loads(p_hbm, p, 2)
-    get_s = loads(s_hbm, s, 3)
-    get_c = loads(c_hbm, cap, 4)
+    free = list(range(send_sem.shape[0]))
+    upper = pl.ds(1, top)
+    get_p = loads(p_hbm, p, 0)
+    get_s0 = loads(s_hbm.at[0], s.at[0], 1)
+    get_c0 = loads(c_hbm.at[0], cap.at[0], 2)
+    get_x = loads(x_hbm, x, 3)
+    get_i = loads(inv_hbm.at[0], inv, 4)
+    get_s = loads(s_hbm.at[upper], s.at[upper], 5)
+    get_c = loads(c_hbm.at[upper], cap.at[upper], 6)
     barrier = pltpu.get_barrier_semaphore()
     for b in range(levels):
         pl.semaphore_signal(barrier, inc=1, device_id=(partner[b],), device_id_type=MESH)
@@ -75,27 +86,30 @@
     z_copy = {}
     c_copy = {}
 
+    get_p.wait()
+    for m in range(1, levels):
+        p_t[m] = p[m].T
+    get_s0.wait()
+    products = dot_nn(p_t[1:levels].reshape(top * rank, seg), s[0]).astype(BF16)
+    get_c0.wait()
+    k0s[...] = dot_nn(products, cap[0]).astype(BF16)
+    pl.semaphore_wait(barrier, levels + 1)
+    k_copy[0] = send(k0s, k0r, 0)
+
     get_x.wait()
     x_t = x[...].T
     get_i.wait()
     st = dot_nt(x_t, inv[...]).astype(BF16)
-    get_p.wait()
     for m in range(levels):
         y = dot_nn(st, p[m]).reshape(2, half, rank)
         y16[m] = y.astype(BF16)
         if m > 0:
             y32[m] = y
-    pl.semaphore_wait(barrier, levels + 1)
     z_copy[0, 0] = send(y16.at[0], y0r, 0)
     z_copy[0, 1] = send(y16.at[pl.ds(1, top), 1 - core], zr0.at[pl.ds(1, top)], 0)
 
-    for m in range(1, levels):
-        p_t[m] = p[m].T
     get_s.wait()
     get_c.wait()
-    products = dot_nn(p_t[1:levels].reshape(top * rank, seg), s[0]).astype(BF16)
-    k0s[...] = dot_nn(products, cap[0]).astype(BF16)
-    k_copy[0] = send(k0s, k0r, 0)
     for l in range(levels - 2, 0, -1):
         products = dot_nn(p_t[l + 1 : levels].reshape((top - l) * rank, seg), s[l])
         if l == 1:
@@ -114,23 +128,21 @@
         if lo >= len(pairs):
             return
         g_copy[b].wait_recv()
-        for i in range(lo, len(pairs)):
+        nxt = first[b + 2]
+        for i in range(len(pairs) - 1, lo - 1, -1):
             old = g32[i, core] if b == 0 else g32[i, 0]
             g = old + gr[b, i].astype(F32)
             g32[i, 0] = g
-            if pairs[i][0] == b + 1:
-                j = pairs[i][1] - (b + 2)
-                kp = dot_nn(g.astype(BF16), cap[b + 1])
-                ks[b + 1, j] = kp.astype(BF16)
-            else:
+            if i >= nxt:
                 gs[b + 1, i, 0] = g.astype(BF16)
-        if b >= 1:
-            n = top - (b + 1)
-            k_copy[b + 1] = send(ks.at[b + 1, pl.ds(0, n)], kr.at[b + 1, pl.ds(0, n)], b + 1)
-        nxt = first[b + 2]
         if nxt < len(pairs):
             rest = pl.ds(nxt, len(pairs) - nxt)
             g_copy[b + 1] = send(gs.at[b + 1, rest, 0], gr.at[b + 1, rest], b + 1)
+        if b >= 1:
+            n = top - (b + 1)
+            for j in range(n):
+                ks[b + 1, j] = dot_nn(g32[lo + j, 0].astype(BF16), cap[b + 1]).astype(BF16)
+            k_copy[b + 1] = send(ks.at[b + 1, pl.ds(0, n)], kr.at[b + 1, pl.ds(0, n)], b + 1)
 
     def k_sum(l):
         n = top - l
@@ -165,6 +177,7 @@
     coef[0] = dot_nt(stacked, cap[0]).astype(BF16).reshape(2, 2, quarter, rank)
     out[...] -= dot_nt(s[0], coef[0].reshape(rhs, rank))
 
+    reap(2)
     z_copy[1, 1].wait_recv()
     c_one = dot_nt(stack(z1s[...], z1r[...], 1), cap[1]).astype(BF16)
     coef[1, core] = c_one.reshape(2, quarter, rank)
@@ -182,12 +195,13 @@
         z32[m] = z
         zs[2, m] = z.astype(BF16)
         z_copy[2, m] = send(zs.at[2, m], zr.at[2, m], 2)
+    g_step(2)
     k_done = k_sum(2)
-    g_step(2)
     c_copy[1].wait_recv()
     out[...] -= dot_nt(s[1], coef[1].reshape(rhs, rank))
 
     for l in range(2, levels):
+        reap(top + 2)
         z_copy[l, l].wait_recv()
         stacked = stack(zs[l, l], zr[l, l], l)
         if l < top:
@@ -203,15 +217,15 @@
         c_copy[l] = [send(mine, mine, 1, diagonal), send(mine, mine, 1), send(mine, mine, 0)]
         if l < top:
             if l + 1 < top:
+                g_step(l + 1)
                 k_done = k_sum(l + 1)
-                g_step(l + 1)
     for l in range(2, levels):
         for copy in c_copy[l]:
             copy.wait_recv()
         if l < top:
             out[...] -= dot_nt(s[l], coef[l].reshape(rhs, rank))
-    for copy in sent:
-        copy.wait_send()
+    reap(0)
+    assert used[0] == recv_sem.shape[0]
     c_last = coef[top].reshape(rhs, rank)
     out[...] -= dot_nt(s[top], c_last)
 
@@ -223,7 +237,9 @@
     quarter = half // 2
     hr = rank // 2
     pairs = max(1, (levels - 2) * (levels - 3) // 2)
-    copies = levels * levels + 6 * levels
+    top = levels - 1
+    copies = 5 + levels + top * (top - 1) // 2 + 3 * (top - 1) + 3 * (top - 2)
+    sends = 3 * levels + 4
     vmem = pltpu.VMEM
     return pl.pallas_call(
         kernel,
@@ -262,8 +278,8 @@
             vmem((pairs, 2, hr, rank), F32),
             vmem((levels - 1, pairs, 2, hr, rank), BF16),
             vmem((levels - 1, pairs, hr, rank), BF16),
-            pltpu.SemaphoreType.DMA((5,)),
-            pltpu.SemaphoreType.DMA((copies,)),
+            pltpu.SemaphoreType.DMA((7,)),
+            pltpu.SemaphoreType.DMA((sends,)),
             pltpu.SemaphoreType.DMA((copies,)),
         ],
         compiler_params=pltpu.CompilerParams(

time: 30.8 us -> 30.4 us (0.987)
  Pallas kernels: 29.8 us -> 29.3 us
    pallas_call x1, Pallas kernels: 29.8 us -> 29.3 us  [on_device(): pl.pallas_call(kernel, name='hodlr_solve', out_shape=pltpu.VMEM((seg, rhs...]
where the time goes in v5:
time: 30.4 us; the launch traced here: 30.2 us
  Pallas kernels  29.3 us (96%)
  local copies, waits for them, and re-layouts  0.88 us (3%)
    pallas_call x1, Pallas kernels, on_device(): pl.pallas_call(kernel, name='hodlr_solve', out_shape=pltpu.VMEM((seg, rhs...  29.3 us
    unnamed x1, local copies, waits for them, and re-layouts  0.88 us

profile of v5, /device:TPU:0, one launch (start us, length us, event | category | flops | bytes accessed | tf_op | source)
XLA Modules:
  0.0 30.2 jit_solution(13933525247676325000)
XLA Ops:
  0.0 29.3 %hodlr_solve.1 = f32[512,384]{1,0:T(8,128)S(1)} custom-call(bf16[512,384]{1,0:T(8,128)(2,1)} %x_hbm.1, bf16[1,512,512]{2,1,0:T(8,128)(2,1)} %inv_hbm.1, bf16[5,512,128]{2,1,0:T(8,128)(2,1)} %p_hbm.1, bf16[5,512,128]{2,1,0:T(8,128)(2,1)} %s_hbm.1, bf16[5,128,256]{2,1,0:T(8,128)(2,1)} %c_hbm.1), custom_call_target="tpu_custom_call" | custom-call | tf_op jit(solution)/shard_map/hodlr_solve/pallas_call | solution.py:244
  29.3 0.9 %copy.7 = f32[512,384]{1,0:T(8,128)} copy(f32[512,384]{1,0:T(8,128)S(1)} %hodlr_solve.1) | data formatting | bytes 1572864

commit v6 on v5

--- a/solution.py
+++ b/solution.py
@@ -142,15 +142,16 @@
             n = top - (b + 1)
             for j in range(n):
                 ks[b + 1, j] = dot_nn(g32[lo + j, 0].astype(BF16), cap[b + 1]).astype(BF16)
-            k_copy[b + 1] = send(ks.at[b + 1, pl.ds(0, n)], kr.at[b + 1, pl.ds(0, n)], b + 1)
+                k_copy[b + 1, j] = send(ks.at[b + 1, j], kr.at[b + 1, j], b + 1)
 
     def k_sum(l):
-        n = top - l
-        k_copy[l].wait_recv()
-        for j in range(n):
+        done = []
+        for j in range(top - l):
+            k_copy[l, j].wait_recv()
             kfull[l, j, core] = (ks[l, j].astype(F32) + kr[l, j].astype(F32)).astype(BF16)
-        mine = kfull.at[l, pl.ds(0, n), core]
-        return send(mine, mine, 0)
+            mine = kfull.at[l, j, core]
+            done.append(send(mine, mine, 0))
+        return done
 
     def stack(own, other, l):
         low = side[l] == 0
@@ -205,9 +206,9 @@
         z_copy[l, l].wait_recv()
         stacked = stack(zs[l, l], zr[l, l], l)
         if l < top:
-            k_done.wait_recv()
             for m in range(l + 1, levels):
                 z_copy[l, m].wait_recv()
+                k_done[m - l - 1].wait_recv()
                 z = z32[m] + zr[l, m].astype(F32) - dot_nt(stacked, kfull[l, m - l - 1].reshape(rank, 2 * rank))
                 z32[m] = z
                 zs[l + 1, m] = z.astype(BF16)
@@ -238,8 +239,8 @@
     hr = rank // 2
     pairs = max(1, (levels - 2) * (levels - 3) // 2)
     top = levels - 1
-    copies = 5 + levels + top * (top - 1) // 2 + 3 * (top - 1) + 3 * (top - 2)
-    sends = 3 * levels + 4
+    copies = 5 + levels + top * (top - 1) // 2 + 3 * (top - 1) + (top - 2) * top
+    sends = 5 * levels
     vmem = pltpu.VMEM
     return pl.pallas_call(
         kernel,

time: 30.4 us -> 30.4 us (level)
  no operation moved by 1% of the time
where the time goes in v6:
time: 30.4 us; the launch traced here: 30.3 us
  Pallas kernels  29.4 us (97%)
  local copies, waits for them, and re-layouts  0.88 us (3%)
    pallas_call x1, Pallas kernels, on_device(): pl.pallas_call(kernel, name='hodlr_solve', out_shape=pltpu.VMEM((seg, rhs...  29.4 us
    unnamed x1, local copies, waits for them, and re-layouts  0.88 us

profile of v6, /device:TPU:0, one launch (start us, length us, event | category | flops | bytes accessed | tf_op | source)
XLA Modules:
  0.0 30.3 jit_solution(11668796531818208659)
XLA Ops:
  0.0 29.4 %hodlr_solve.1 = f32[512,384]{1,0:T(8,128)S(1)} custom-call(bf16[512,384]{1,0:T(8,128)(2,1)} %x_hbm.1, bf16[1,512,512]{2,1,0:T(8,128)(2,1)} %inv_hbm.1, bf16[5,512,128]{2,1,0:T(8,128)(2,1)} %p_hbm.1, bf16[5,512,128]{2,1,0:T(8,128)(2,1)} %s_hbm.1, bf16[5,128,256]{2,1,0:T(8,128)(2,1)} %c_hbm.1), custom_call_target="tpu_custom_call" | custom-call | tf_op jit(solution)/shard_map/hodlr_solve/pallas_call | solution.py:245
  29.4 0.9 %copy.7 = f32[512,384]{1,0:T(8,128)} copy(f32[512,384]{1,0:T(8,128)S(1)} %hodlr_solve.1) | data formatting | bytes 1572864
